TPU v7x, 32 devices: a whole 2x2x4 slice. The times are simulated.
32 devices in a mesh: dp: 16 (over z, y, x), tensor: 2 (over core).
Axes of the slice: x: 2, y: 2, z: 4, core: 2. Of those that a mesh axis runs over, the one named last changes fastest.
Arguments:
- image_tokens: bfloat16 [32, 577, 1024], P('dp'), may hold values from -6 to 6
- first_gain: float32 [1024], replicated, may hold values from 0.5 to 1.5
- first_shift: float32 [1024], replicated, may hold values from -1.5 to 1.5
- w_qkv: bfloat16 [1024, 3, 1024], P(None, None, 'tensor'), may hold values from -8 to 8, as said below
- query_value_bias: float32 [2, 1024], P(None, 'tensor'), may hold values from -1.5 to 1.5
- w_out: bfloat16 [1024, 1024], P('tensor'), may hold values from -1.5 to 1.5
- out_bias: float32 [1024], replicated, may hold values from -1.5 to 1.5
- second_gain: float32 [1024], replicated, may hold values from 0.5 to 1.5
- second_shift: float32 [1024], replicated, may hold values from -1.5 to 1.5
- w_up: bfloat16 [1024, 4096], P(None, 'tensor'), may hold values from -0.1875 to 0.1875
- up_bias: float32 [4096], P('tensor'), may hold values from -1.5 to 1.5
- w_down: bfloat16 [4096, 1024], P('tensor'), may hold values from -0.09375 to 0.09375
- down_bias: float32 [1024], replicated, may hold values from -1.5 to 1.5
- cotangent: bfloat16 [32, 577, 1024], P('dp'), may hold values from -6 to 6
Outputs:
- layer_output: bfloat16 [32, 577, 1024], P('dp')
- grad_input: bfloat16 [32, 577, 1024], P('dp')
- grad_first_gain: float32 [1024], replicated
- grad_first_shift: float32 [1024], replicated
- grad_qkv: float32 [1024, 3, 1024], P(None, None, 'tensor')
- grad_query_value_bias: float32 [2, 1024], P(None, 'tensor')
- grad_out: float32 [1024, 1024], P('tensor')
- grad_out_bias: float32 [1024], replicated
- grad_second_gain: float32 [1024], replicated
- grad_second_shift: float32 [1024], replicated
- grad_up: float32 [1024, 4096], P(None, 'tensor')
- grad_up_bias: float32 [4096], P('tensor')
- grad_down: float32 [4096, 1024], P('tensor')
- grad_down_bias: float32 [1024], replicated
Inputs may be any that keep to these rules, and one draw needn't show every extreme that they name: `w_qkv`: independent entries of order 1024^(-1/2) in every column.
All inputs are finite; a program needn't handle non-finite values.
Results may differ from a plain program's by a relative error of at most 0.012.
Values sent between devices are 32-bit elements; how exact they have to be, the bound alone decides.
A program may use at most 192 MiB of HBM per device.

v0:
```python
import jax
import jax.numpy as jnp
from jax import lax
from jax.sharding import PartitionSpec as P

HEAD_DIM = 64


EPSILON = 1e-06
ROOT_HALF = 0.7071067811865476
DENSITY_SCALE = 0.3989422804014327


def norm_forward(inputs, gain_row, shift_row):
    centred = inputs - jnp.mean(inputs, -1, keepdims=True)
    inverse = lax.rsqrt(jnp.mean(centred * centred, -1, keepdims=True) + EPSILON)
    normed = centred * inverse
    return (normed * gain_row + shift_row, normed, inverse)


def norm_backward(upstream, normed, inverse, gain_row):
    scaled = upstream * gain_row
    centred_grad = (
        scaled
        - jnp.mean(scaled, -1, keepdims=True)
        - normed * jnp.mean(scaled * normed, -1, keepdims=True)
    )
    return (centred_grad * inverse, jnp.sum(upstream * normed, 0), jnp.sum(upstream, 0))


def gelu_slope(pre_act):
    normal_cdf = 0.5 * (1.0 + lax.erf(pre_act * ROOT_HALF))
    density = jnp.exp(-0.5 * pre_act * pre_act) * DENSITY_SCALE
    return normal_cdf + pre_act * density


def attend_image(image_block):
    queries, key_rows, values = image_block
    score_scale = HEAD_DIM ** (-0.5)
    scores = (
        jnp.einsum("qhd,khd->hqk", queries, key_rows, preferred_element_type=jnp.float32)
        * score_scale
    )
    row_top = jnp.max(scores, -1, keepdims=True)
    log_total = row_top + jnp.log(jnp.sum(jnp.exp(scores - row_top), -1, keepdims=True))
    prob_low = jnp.exp(scores - log_total).astype(jnp.bfloat16)
    context = jnp.einsum("hqk,khd->qhd", prob_low, values, preferred_element_type=jnp.float32)
    return (context.astype(jnp.bfloat16), log_total)


def attend_backward(image_block):
    queries, key_rows, values, log_total, d_context = image_block
    score_scale = HEAD_DIM ** (-0.5)
    scores = (
        jnp.einsum("qhd,khd->hqk", queries, key_rows, preferred_element_type=jnp.float32)
        * score_scale
    )
    prob_full = jnp.exp(scores - log_total)
    d_prob = jnp.einsum("qhd,khd->hqk", d_context, values, preferred_element_type=jnp.float32)
    row_inner = jnp.sum(prob_full * d_prob, -1, keepdims=True)
    d_scores = (prob_full * (d_prob - row_inner)).astype(jnp.bfloat16)
    d_queries = (
        jnp.einsum("hqk,khd->qhd", d_scores, key_rows, preferred_element_type=jnp.float32)
        * score_scale
    ).astype(jnp.bfloat16)
    d_keys = (
        jnp.einsum("hqk,qhd->khd", d_scores, queries, preferred_element_type=jnp.float32)
        * score_scale
    ).astype(jnp.bfloat16)
    d_values = jnp.einsum(
        "hqk,qhd->khd",
        prob_full.astype(jnp.bfloat16),
        d_context,
        preferred_element_type=jnp.float32,
    ).astype(jnp.bfloat16)
    return (d_queries, d_keys, d_values)


def body(
    image_tokens,
    first_gain,
    first_shift,
    w_qkv,
    query_value_bias,
    w_out,
    out_bias,
    second_gain,
    second_shift,
    w_up,
    up_bias,
    w_down,
    down_bias,
    cotangent,
):
    images, length, model_width = image_tokens.shape
    local_cols = w_qkv.shape[2]
    heads_here = local_cols // HEAD_DIM
    shaped = (images, length, heads_here, HEAD_DIM)
    inputs = image_tokens.astype(jnp.float32).reshape(images * length, model_width)
    first_normed, hat_first, inverse_first = norm_forward(inputs, first_gain, first_shift)
    first_normed = first_normed.astype(jnp.bfloat16)
    qkv_matrix = w_qkv.reshape(model_width, 3 * local_cols)
    joined = jnp.dot(first_normed, qkv_matrix, preferred_element_type=jnp.float32).reshape(
        -1, 3, local_cols
    )
    queries = (joined[:, 0] + query_value_bias[0]).astype(jnp.bfloat16).reshape(shaped)
    key_rows = joined[:, 1].astype(jnp.bfloat16).reshape(shaped)
    values = (joined[:, 2] + query_value_bias[1]).astype(jnp.bfloat16).reshape(shaped)
    context, log_total = lax.map(attend_image, (queries, key_rows, values))
    context_rows = context.reshape(-1, local_cols)
    attention = lax.psum(jnp.dot(context_rows, w_out, preferred_element_type=jnp.float32), "tensor")
    hidden_in = inputs + attention + out_bias
    second_normed, hat_second, inverse_second = norm_forward(hidden_in, second_gain, second_shift)
    second_normed = second_normed.astype(jnp.bfloat16)
    pre_act = jnp.dot(second_normed, w_up, preferred_element_type=jnp.float32) + up_bias
    hidden_act = (pre_act * 0.5 * (1.0 + lax.erf(pre_act * ROOT_HALF))).astype(jnp.bfloat16)
    branch = lax.psum(jnp.dot(hidden_act, w_down, preferred_element_type=jnp.float32), "tensor")
    layer_output = (hidden_in + branch + down_bias).astype(jnp.bfloat16).reshape(image_tokens.shape)
    d_out = cotangent.astype(jnp.float32).reshape(-1, model_width)
    d_out_low = d_out.astype(jnp.bfloat16)
    grad_down_bias = jnp.sum(d_out, 0)
    grad_down = jnp.einsum("rf,rd->fd", hidden_act, d_out_low, preferred_element_type=jnp.float32)
    d_hidden_act = jnp.einsum("rd,fd->rf", d_out_low, w_down, preferred_element_type=jnp.float32)
    d_pre = (d_hidden_act * gelu_slope(pre_act)).astype(jnp.bfloat16)
    grad_up = jnp.einsum("rd,rf->df", second_normed, d_pre, preferred_element_type=jnp.float32)
    grad_up_bias = jnp.sum(d_pre.astype(jnp.float32), 0)
    d_second = lax.psum(
        jnp.einsum("rf,df->rd", d_pre, w_up, preferred_element_type=jnp.float32), "tensor"
    )
    d_mid, grad_second_gain, grad_second_shift = norm_backward(
        d_second, hat_second, inverse_second, second_gain
    )
    d_hidden = d_out + d_mid
    grad_out_bias = jnp.sum(d_hidden, 0)
    d_hidden_low = d_hidden.astype(jnp.bfloat16)
    grad_out = jnp.einsum(
        "rc,rd->cd", context_rows, d_hidden_low, preferred_element_type=jnp.float32
    )
    d_context = (
        jnp.einsum("rd,cd->rc", d_hidden_low, w_out, preferred_element_type=jnp.float32)
        .astype(jnp.bfloat16)
        .reshape(shaped)
    )
    d_queries, d_keys, d_values = lax.map(
        attend_backward, (queries, key_rows, values, log_total, d_context)
    )
    d_queries = d_queries.reshape(-1, local_cols)
    d_values = d_values.reshape(-1, local_cols)
    d_joined = jnp.stack([d_queries, d_keys.reshape(-1, local_cols), d_values], axis=1).reshape(
        -1, 3 * local_cols
    )
    grad_qkv = jnp.einsum(
        "rd,rc->dc", first_normed, d_joined, preferred_element_type=jnp.float32
    ).reshape(model_width, 3, local_cols)
    grad_query_value_bias = jnp.stack(
        [jnp.sum(d_queries.astype(jnp.float32), 0), jnp.sum(d_values.astype(jnp.float32), 0)]
    )
    d_first = lax.psum(
        jnp.einsum("rc,dc->rd", d_joined, qkv_matrix, preferred_element_type=jnp.float32), "tensor"
    )
    d_low, grad_first_gain, grad_first_shift = norm_backward(
        d_first, hat_first, inverse_first, first_gain
    )
    grad_input = (d_hidden + d_low).astype(jnp.bfloat16).reshape(image_tokens.shape)
    (
        grad_first_gain,
        grad_first_shift,
        grad_qkv,
        grad_query_value_bias,
        grad_out,
        grad_out_bias,
        grad_second_gain,
        grad_second_shift,
        grad_up,
        grad_up_bias,
        grad_down,
        grad_down_bias,
    ) = lax.psum(
        (
            grad_first_gain,
            grad_first_shift,
            grad_qkv,
            grad_query_value_bias,
            grad_out,
            grad_out_bias,
            grad_second_gain,
            grad_second_shift,
            grad_up,
            grad_up_bias,
            grad_down,
            grad_down_bias,
        ),
        "dp",
    )
    return (
        layer_output,
        grad_input,
        grad_first_gain,
        grad_first_shift,
        grad_qkv,
        grad_query_value_bias,
        grad_out,
        grad_out_bias,
        grad_second_gain,
        grad_second_shift,
        grad_up,
        grad_up_bias,
        grad_down,
        grad_down_bias,
    )


def solution(mesh):
    in_specs = (
        P("dp", None, None),
        P(),
        P(),
        P(None, None, "tensor"),
        P(None, "tensor"),
        P("tensor", None),
        P(),
        P(),
        P(),
        P(None, "tensor"),
        P("tensor"),
        P("tensor", None),
        P(),
        P("dp", None, None),
    )
    out_specs = (
        P("dp", None, None),
        P("dp", None, None),
        P(),
        P(),
        P(None, None, "tensor"),
        P(None, "tensor"),
        P("tensor", None),
        P(),
        P(),
        P(),
        P(None, "tensor"),
        P("tensor"),
        P("tensor", None),
        P(),
    )
    return jax.shard_map(body, mesh=mesh, in_specs=in_specs, out_specs=out_specs, check_vma=False)
```

profile of v0, /device:TPU:0, one launch (start us, length us, event | category | flops | bytes accessed | tf_op | source)
XLA Modules:
  0.0 1035.2 jit_solution(15342603883010051172)
XLA Ops:
  27.3 5.8 fusion.65
  66.5 17.5 %while.26 = (s32[]{:T(128)}, bf16[2,577,8,64]{1,3,2,0:T(8,128)(2,1)}, f32[2,8,577,1]{2,1,3,0:T(8,128)S(1)}, bf16[2,577,8,64]{1,3,2,0:T(8,128)(2,1)}, bf16[2,577,...) while((s32[]{:T(128)}, bf16[2,577,8,64]{1,3,2,0:T(8,128)(2,1)}, ...), condition=%wide.region_5.6_spmd, body=%wide.region_2.5_spmd.sunk | while | flops 703436800 | bytes 50229580 | solution.py:109
  104.9 6.0 reshape.217
  116.1 12.6 %all-reduce.8.cloned.1.call-done = f32[1154,1024]{1,0:T(8,128)} async-done(((f32[1154,1024]{1,0:T(8,128)}), f32[1154,1024]{1,0:T(8,128)}) %all-reduce.8.cloned.1.call-update) | async-done | bytes 4726800 | tf_op jit(solution)/shard_map/psum | solution.py:111
  137.1 9.7 multiply_convert_fusion.1
  146.8 10.7 %convert_reduce_fusion = (f32[2048]{0:T(1024)}, bf16[1154,2048]{1,0:T(8,128)(2,1)S(1)}) fusion(f32[1154,2048]{1,0:T(8,128)} %get-tuple-element.284, bf16[2048,1024]{1,0:T(8,128)(2,1)S(1)} %copy-done.53, f32[1154,1024]{1,0:T(8,128)S(1)} %bitcast.149), kind=kOutput, calls=%fused_computation.68 | convolution fusion | flops 4869767168 | bytes 23109632 | tf_op jit(solution)/shard_map/rd,fd->rf/dot_general | solution.py:123
  159.6 6.8 fusion.79
  166.5 10.2 fusion.78
  176.7 20.0 %all-reduce.10.cloned.1.call-done = f32[1154,1024]{1,0:T(8,128)} async-done(((f32[1154,1024]{1,0:T(8,128)}), f32[1154,1024]{1,0:T(8,128)}) %all-reduce.10.cloned.1.call-update) | async-done | bytes 4726800 | tf_op jit(solution)/shard_map/psum | solution.py:127
  196.7 5.7 multiply_reduce_fusion.2
  221.9 44.3 %while.27 = (s32[]{:T(128)}, bf16[2,577,8,64]{1,3,2,0:T(8,128)(2,1)}, bf16[2,577,8,64]{1,3,2,0:T(8,128)(2,1)}, bf16[2,577,8,64]{1,3,2,0:T(8,128)(2,1)}, bf16[2,5...) while((s32[]{:T(128)}, ...), condition=%wide.region_15.16_spmd, body=%wide.region_13.15_spmd.sunk | while | flops 1738030080 | bytes 133056176 | solution.py:144
  227.6 5.8 multiply_reduce_fusion.13
  233.4 6.4 multiply_convert_fusion.3
  249.7 5.8 multiply_reduce_fusion.13
  255.5 6.4 multiply_convert_fusion.3
  299.4 11.6 %fusion.70 = f32[2048,1024]{1,0:T(8,128)} fusion(bf16[1154,2048]{1,0:T(8,128)(2,1)} %get-tuple-element.283, f32[1154,1024]{1,0:T(8,128)} %reshape.217), kind=kOutput, calls=%fused_computation.104 | convolution fusion | flops 4841408512 | bytes 17842176 | tf_op jit(solution)/shard_map/rf,rd->fd/dot_general | solution.py:122
  311.0 13.6 %fusion.73 = f32[1024,2048]{1,0:T(8,128)} fusion(bf16[1154,2048]{1,0:T(8,128)(2,1)} %copy-done.57, f32[1154,1024]{1,0:T(8,128)} %copy-done.2, f32[1024]{0:T(1024)S(1)} %copy-done.56, f32[1024]{0:T(1024)S(1)} %copy-done.43, f32[1154]{0:T(1024)S(1)} %copy-done.39, f32[1154]{0:T(1024)S(1)} %copy-done.37), kind=kOutput, calls=%fused_computation.122 | convolution fusion | flops 4846135296 | bytes 17859600 | tf_op jit(solution)/shard_map/rd,rf->df/dot_general | solution.py:125
  324.7 6.0 fusion.67
  330.6 6.8 fusion.63
  344.8 6.5 add_convert_fusion.1
  357.3 6.0 multiply_reduce_fusion.3
  374.6 82.0 %all-reduce = (f32[1024]{0:T(1024)}, f32[1024]{0:T(1024)}, f32[2,512]{1,0:T(2,128)}, f32[1024]{0:T(1024)}, f32[1024]{0:T(1024)}, /*index=5*/f32[1024]{0:T(1024)}, f32[2048]{0:T(1024)}, f32[1024]{0:T(1024)}) all-reduce(f32[1024]{0:T(1024)S(1)} %get-tuple-element.219, ...), channel_id=1, replica_groups=mesh['dp'=16,'tensor'=2] {'dp'}, use_global_device_ids=true, to_apply=%region_20.21 | all-reduce | flops 9216 | bytes 73728 | tf_op jit(solution)/shard_map/psum | solution.py:178
  456.5 554.2 %all-reduce.12.cloned.1.call-done = (f32[1024,3,512]{2,0,1:T(8,128)}, f32[512,1024]{1,0:T(8,128)}, f32[1024,2048]{1,0:T(8,128)}, f32[2048,1024]{1,0:T(8,128)}) async-done(((f32[1024,3,512]{2,0,1:T(8,128)}, f32[512,1024]{1,0:T(8,128)}, f32[1024,2048]{1,0:T(8,128)}, f32[2048,1024]{1,0:T(8,128)}), (f32[1024,3,512]{2,0,1:T(8,128)}, f32[512,1024]{1,0:T(8,128)}, f32[1024,2048]{1,0:T(8,128)}, ...) | async-done | bytes 25165840 | tf_op jit(solution)/shard_map/psum | solution.py:178
  1010.7 6.9 copy.199
  (255 shorter events, 214.8 us)
Async XLA Ops:
  7.2 84.8 %copy-start = (bf16[512,1024]{1,0:T(8,128)(2,1)S(1)}, bf16[512,1024]{1,0:T(8,128)(2,1)}, u32[]{:S(2)}) copy-start(bf16[512,1024]{1,0:T(8,128)(2,1)} %param.23) | copy-start | bytes 3145732
  7.2 121.5 %all-reduce.8.cloned.1.call-start = ((), (), s32[]{:S(2)}) async-start(), calls=%async_computation | async-start | bytes 9502720 | tf_op jit(solution)/shard_map/psum | solution.py:111
  11.1 8.8 copy-start.23
  38.4 8.9 copy-start.25
  84.0 12.9 %copy-start.34 = (f32[2,8,577,1]{2,1,3,0:T(8,128)}, f32[2,8,577,1]{2,1,3,0:T(8,128)S(1)}, u32[]{:S(2)}) copy-start(f32[2,8,577,1]{2,1,3,0:T(8,128)S(1)} %get-tuple-element.420) | copy-start | bytes 110788
  96.9 99.8 %all-reduce.10.cloned.1.call-start = ((), (), s32[]{:S(2)}) async-start(), calls=%async_computation.1 | async-start | bytes 9502720 | tf_op jit(solution)/shard_map/psum | solution.py:127
  110.9 17.8 %copy-start.48 = (f32[1024]{0:T(1024)S(1)}, f32[1024]{0:T(1024)}, u32[]{:S(2)}) copy-start(f32[1024]{0:T(1024)} %param.24) | copy-start | bytes 12292
  133.1 13.7 %copy-start.2 = (f32[1154,1024]{1,0:T(8,128)}, f32[1154,1024]{1,0:T(8,128)S(1)}, u32[]{:S(2)}) copy-start(f32[1154,1024]{1,0:T(8,128)S(1)} %get-tuple-element.276) | copy-start | bytes 14180356
  133.2 69.3 %copy-start.36 = (f32[1154]{0:T(1024)}, f32[1154]{0:T(1024)S(1)}, u32[]{:S(2)}) copy-start(f32[1154]{0:T(1024)S(1)} %broadcast_multiply_fusion.5) | copy-start | bytes 13852
  133.2 13.6 %slice-start.2 = ((s8[4751360]{0:T(1024)(128)(4,1)}), s8[4194304]{0:T(1024)(128)(4,1)S(1)}, s32[]{:S(2)}) async-start(s8[4751360]{0:T(1024)(128)(4,1)} %bitcast.148), calls=%async_computation.6 | async-start | bytes 8388608
  137.0 65.4 %copy-start.38 = (f32[1154]{0:T(1024)}, f32[1154]{0:T(1024)S(1)}, u32[]{:S(2)}) copy-start(f32[1154]{0:T(1024)S(1)} %add_rsqrt_fusion.1) | copy-start | bytes 13852
  137.0 9.8 slice-start.3
  137.0 9.8 copy-start.53
  166.4 178.3 %all-reduce.14.cloned.1.call-start = ((), (), s32[]{:S(2)}) async-start(), calls=%async_computation.3 | async-start | bytes 19005440 | tf_op jit(solution)/shard_map/psum | solution.py:117
  211.5 10.4 %copy-start.35 = (f32[2,8,577,1]{2,1,3,0:T(8,128)S(1)}, f32[2,8,577,1]{2,1,3,0:T(8,128)}, u32[]{:S(2)}) copy-start(f32[2,8,577,1]{2,1,3,0:T(8,128)} %copy-done.34) | copy-start | bytes 110788
  299.3 11.7 %copy-start.37 = (f32[1154]{0:T(1024)S(1)}, f32[1154]{0:T(1024)}, u32[]{:S(2)}) copy-start(f32[1154]{0:T(1024)} %copy-done.36) | copy-start | bytes 13852
  299.3 11.7 %copy-start.39 = (f32[1154]{0:T(1024)S(1)}, f32[1154]{0:T(1024)}, u32[]{:S(2)}) copy-start(f32[1154]{0:T(1024)} %copy-done.38) | copy-start | bytes 13852
  299.3 11.7 %copy-start.43 = (f32[1024]{0:T(1024)S(1)}, f32[1024]{0:T(1024)}, u32[]{:S(2)}) copy-start(f32[1024]{0:T(1024)} %param.25) | copy-start | bytes 12292
  299.3 11.6 %copy-start.56 = (f32[1024]{0:T(1024)S(1)}, f32[1024]{0:T(1024)}, u32[]{:S(2)}) copy-start(f32[1024]{0:T(1024)} %param.26) | copy-start | bytes 12292
  299.4 711.4 %all-reduce.12.cloned.1.call-start = ((), (), s32[]{:S(2)}) async-start(), calls=%async_computation.2 | async-start | bytes 50331648 | tf_op jit(solution)/shard_map/psum | solution.py:178
  311.0 13.7 %copy-start.22 = (bf16[1154,512]{0,1:T(8,128)(2,1)S(1)}, bf16[1154,512]{0,1:T(8,128)(2,1)}, u32[]{:S(2)}) copy-start(bf16[1154,512]{0,1:T(8,128)(2,1)} %reshape.215) | copy-start | bytes 3545092
  353.4 9.9 slice-start
  1010.7 8.6 copy-start.17
  1019.3 9.2 copy-start.1
  (56 other events, 224.9 us)
Sparse Core Ops, SparseCore 0:
  97.0 31.6 all-reduce.7
  166.6 30.0 all-reduce.9
  299.4 42.1 all-reduce.13
  349.0 661.6 all-reduce.11
where the time goes:
time: 1040 us
  waiting for transfers between devices  587 us (56%)
  local copies, waits for them, and re-layouts  145 us (14%)
  matrix products  133 us (13%)
  blocking collectives  82 us (8%)
  other arithmetic  73.4 us (7%)
  between operations  14.5 us (1%)
    psum x1, waiting for transfers between devices, body(): lax.psum((grad_first_gain, grad_first_shift, grad_qkv, grad_query_value_b...  554 us
    psum x1, blocking collectives, body(): lax.psum((grad_first_gain, grad_first_shift, grad_qkv, grad_query_value_b...  82 us
    unnamed x115, local copies, waits for them, and re-layouts  45 us
    another operation x7, local copies, waits for them, and re-layouts, body(): jnp.stack([d_queries, d_keys.reshape(-1, local_cols), d_values], axis=1)  22.9 us
  transfers between devices with their start and end apart: 4, of which 3 were waited for; matrix products, arithmetic and copies ran while one was open for 10% of the time, Pallas kernels for 0%

commit v1 on v0

v1 whole, which is shorter than its diff:
```python
import functools

import jax
import jax.numpy as jnp
from jax import lax
from jax.experimental import pallas as pl
from jax.experimental.pallas import tpu as pltpu
from jax.sharding import PartitionSpec as P

HEAD_DIM = 64
LANES = 128
EPSILON = 1e-06
ROOT_HALF = 0.7071067811865476
DENSITY_SCALE = 0.3989422804014327
MASKED = -1e30
F32 = jnp.float32
BF16 = jnp.bfloat16


def dot(a, b):
    return jnp.dot(a, b, preferred_element_type=F32)


def dot_nt(a, b):
    return lax.dot_general(a, b, (((1,), (1,)), ((), ())), preferred_element_type=F32)


def dot_tn(a, b):
    return lax.dot_general(a, b, (((0,), (0,)), ((), ())), preferred_element_type=F32)


def padded_rows(length):
    return -(-length // 16) * 16


def normalise(rows):
    centred = rows - jnp.mean(rows, -1, keepdims=True)
    inverse = lax.rsqrt(jnp.mean(centred * centred, -1, keepdims=True) + EPSILON)
    return centred * inverse, inverse


def norm_backward(upstream, normed, inverse, gain_row):
    scaled = upstream * gain_row
    return inverse * (
        scaled
        - jnp.mean(scaled, -1, keepdims=True)
        - normed * jnp.mean(scaled * normed, -1, keepdims=True)
    )


def store_rows(ref, rows):
    length, total = rows.shape[0], ref.shape[0]
    if length < total:
        start = length // 16 * 16
        ref[start:total, :] = jnp.zeros((total - start, ref.shape[1]), ref.dtype)
    ref[0:length, :] = rows.astype(ref.dtype)


def whole(shape):
    return pl.BlockSpec(shape, lambda *_: (0,) * len(shape))


def image_spec(shape, image):
    return pl.BlockSpec((None,) + tuple(shape[1:]), lambda *_: (image, 0, 0))


def cost(flops, moved, transcendentals=0):
    return pl.CostEstimate(
        flops=int(flops), bytes_accessed=int(moved), transcendentals=int(transcendentals)
    )


def head_lanes(rows, head):
    lane = lax.broadcasted_iota(jnp.int32, rows.shape, 1)
    return jnp.where((lane < HEAD_DIM) == (head == 0), rows, jnp.zeros_like(rows))


def softmax_rows(queries, key_rows, length):
    scores = dot_nt(queries, key_rows)
    column = lax.broadcasted_iota(jnp.int32, scores.shape, 1)
    scores = jnp.where(column < length, scores, MASKED)
    exps = jnp.exp(scores - jnp.max(scores, -1, keepdims=True))
    return exps * (1.0 / jnp.sum(exps, -1, keepdims=True))


def attention_kernel(
    length, x_ref, gain_ref, shift_ref, wqkv_ref, bias_ref, wout_ref, xn_ref, qkv_ref, ctx_ref, part_ref
):
    normed, _ = normalise(x_ref[...].astype(F32))
    store_rows(xn_ref, normed * gain_ref[...] + shift_ref[...])
    qkv_ref[...] = (dot(xn_ref[...], wqkv_ref[...]) + bias_ref[...]).astype(BF16)
    width = ctx_ref.shape[1]

    def pair(index, carry):
        start = pl.multiple_of(index * LANES, LANES)
        queries = qkv_ref[:, pl.ds(start, LANES)] * BF16(HEAD_DIM ** (-0.5))
        key_rows = qkv_ref[:, pl.ds(start + width, LANES)]
        values = qkv_ref[:, pl.ds(start + 2 * width, LANES)]
        total = jnp.zeros((queries.shape[0], LANES), F32)
        for head in range(2):
            prob = softmax_rows(head_lanes(queries, head), key_rows, length)
            total = total + dot(prob.astype(BF16), head_lanes(values, head))
        ctx_ref[:, pl.ds(start, LANES)] = total.astype(BF16)
        return carry

    lax.fori_loop(0, width // LANES, pair, 0)
    part_ref[...] = dot(ctx_ref[...], wout_ref[...])


def attention_forward(image, tokens, gain, shift, wqkv, bias, w_out):
    _, length, model = tokens.shape
    width = w_out.shape[0]
    rows = padded_rows(length)
    shapes = [((rows, model), BF16), ((rows, 3 * width), BF16), ((rows, width), BF16), ((rows, model), F32)]
    return pl.pallas_call(
        functools.partial(attention_kernel, length),
        grid=(1,),
        in_specs=[
            image_spec(tokens.shape, image),
            whole(gain.shape),
            whole(shift.shape),
            whole(wqkv.shape),
            whole(bias.shape),
            whole(w_out.shape),
        ],
        out_specs=[whole(s) for s, _ in shapes],
        out_shape=[jax.ShapeDtypeStruct(s, d) for s, d in shapes],
        cost_estimate=cost(2 * rows * model * 4 * width + 16 * rows * rows * width, 12e6, rows * rows * 8),
        name="attention_forward",
    )(tokens, gain, shift, wqkv, bias, w_out)


def feed_kernel(
    x_ref, own_ref, peer_ref, obias_ref, gain_ref, shift_ref, wup_ref, ubias_ref, wdown_ref, cot_ref,
    hid_ref, sn_ref, act_ref, dpre_ref, dout_ref, usum_ref, dsum_ref,
):
    @pl.when(pl.program_id(0) == 0)
    def _():
        length = x_ref.shape[0]
        hid = x_ref[...].astype(F32) + (own_ref[0:length, :] + peer_ref[0:length, :]) + obias_ref[...]
        store_rows(hid_ref, hid)
        normed, _ = normalise(hid)
        store_rows(sn_ref, normed * gain_ref[...] + shift_ref[...])
        store_rows(dout_ref, cot_ref[...])
        dsum_ref[...] = jnp.sum(cot_ref[...].astype(F32), 0, keepdims=True)

    pre = dot(sn_ref[...], wup_ref[...]) + ubias_ref[...]
    upstream = dot_nt(dout_ref[...], wdown_ref[...])
    cdf = 0.5 * (1.0 + lax.erf(pre * ROOT_HALF))
    act_ref[...] = (pre * cdf).astype(BF16)
    slope = cdf + pre * (jnp.exp(-0.5 * pre * pre) * DENSITY_SCALE)
    dpre = (upstream * slope).astype(BF16)
    dpre_ref[...] = dpre
    usum_ref[...] = jnp.sum(dpre.astype(F32), 0, keepdims=True)


def feed_forward(image, tokens, own, peer, out_bias, gain, shift, w_up, up_bias, w_down, cotangent):
    rows, model = own.shape
    units = w_up.shape[1]
    tile = min(512, units)
    shapes = [
        ((rows, model), F32),
        ((rows, model), BF16),
        ((rows, units), BF16),
        ((rows, units), BF16),
        ((rows, model), BF16),
        ((1, units), F32),
        ((1, model), F32),
    ]
    return pl.pallas_call(
        feed_kernel,
        grid=(units // tile,),
        in_specs=[
            image_spec(tokens.shape, image),
            whole(own.shape),
            whole(peer.shape),
            whole(out_bias.shape),
            whole(gain.shape),
            whole(shift.shape),
            pl.BlockSpec((model, tile), lambda t: (0, t)),
            pl.BlockSpec((1, tile), lambda t: (0, t)),
            pl.BlockSpec((tile, model), lambda t: (t, 0)),
            image_spec(cotangent.shape, image),
        ],
        out_specs=[
            whole((rows, model)),
            whole((rows, model)),
            pl.BlockSpec((rows, tile), lambda t: (0, t)),
            pl.BlockSpec((rows, tile), lambda t: (0, t)),
            whole((rows, model)),
            pl.BlockSpec((1, tile), lambda t: (0, t)),
            whole((1, model)),
        ],
        out_shape=[jax.ShapeDtypeStruct(s, d) for s, d in shapes],
        cost_estimate=cost(4 * rows * model * units, 25e6, 2 * rows * units),
        name="feed_forward",
    )(tokens, own, peer, out_bias, gain, shift, w_up, up_bias, w_down, cotangent)


def weight_grad_kernel(order_ref, left0_ref, left1_ref, right0_ref, right1_ref, first_ref, second_ref):
    for step, out_ref in enumerate((first_ref, second_ref)):

        @pl.when(pl.program_id(0) == step)
        def _():
            out_ref[...] = dot_tn(left0_ref[...], right0_ref[...]) + dot_tn(left1_ref[...], right1_ref[...])


def weight_grad(order, left, right, tile, name):
    rows = left[0].shape[0]
    columns = right[0].shape[1]
    left_spec = pl.BlockSpec((rows, tile), lambda t, order: (0, order[t]))
    return pl.pallas_call(
        weight_grad_kernel,
        grid_spec=pltpu.PrefetchScalarGridSpec(
            num_scalar_prefetch=1,
            grid=(2,),
            in_specs=[left_spec, left_spec, whole(right[0].shape), whole(right[1].shape)],
            out_specs=[whole((tile, columns))] * 2,
        ),
        out_shape=[jax.ShapeDtypeStruct((tile, columns), F32)] * 2,
        cost_estimate=cost(8 * rows * columns * tile, 4 * rows * columns + 8 * tile * (rows + columns)),
        name=name,
    )(order, left[0], left[1], right[0], right[1])


def product_kernel(transposed, left_ref, right_ref, out_ref):
    out_ref[...] = (dot_nt if transposed else dot)(left_ref[...], right_ref[...])


def product(left, right, transposed, name):
    rows, depth = left.shape
    columns = right.shape[0] if transposed else right.shape[1]
    tile = min(512, columns)
    right_block = (tile, depth) if transposed else (depth, tile)
    return pl.pallas_call(
        functools.partial(product_kernel, transposed),
        grid=(columns // tile,),
        in_specs=[
            whole(left.shape),
            pl.BlockSpec(right_block, (lambda t: (t, 0)) if transposed else (lambda t: (0, t))),
        ],
        out_specs=pl.BlockSpec((rows, tile), lambda t: (0, t)),
        out_shape=jax.ShapeDtypeStruct((rows, columns), F32),
        cost_estimate=cost(2 * rows * depth * columns, 2 * rows * depth + 2 * depth * columns + 4 * rows * columns),
        name=name,
    )(left, right)


def attention_back_kernel(
    length, hid_ref, own_ref, peer_ref, gain_ref, dout_ref, wout_ref, qkv_ref,
    dhid_ref, dlow_ref, dqkv_ref, sums_ref, bsums_ref, dctx_ref,
):
    normed, inverse = normalise(hid_ref[...])
    upstream = own_ref[...] + peer_ref[...]
    dhid = dout_ref[...].astype(F32) + norm_backward(upstream, normed, inverse, gain_ref[...])
    dhid_ref[...] = dhid
    dlow_ref[...] = dhid.astype(BF16)
    sums_ref[0:1, :] = jnp.sum(upstream * normed, 0, keepdims=True)
    sums_ref[1:2, :] = jnp.sum(upstream, 0, keepdims=True)
    sums_ref[2:3, :] = jnp.sum(dhid, 0, keepdims=True)
    dctx_ref[...] = dot_nt(dlow_ref[...], wout_ref[...]).astype(BF16)
    width = dctx_ref.shape[1]
    scale = HEAD_DIM ** (-0.5)

    def pair(index, carry):
        start = pl.multiple_of(index * LANES, LANES)
        queries = qkv_ref[:, pl.ds(start, LANES)]
        key_rows = qkv_ref[:, pl.ds(start + width, LANES)]
        values = qkv_ref[:, pl.ds(start + 2 * width, LANES)]
        dctx = dctx_ref[:, pl.ds(start, LANES)]
        dq = jnp.zeros(queries.shape, F32)
        dk = jnp.zeros(queries.shape, F32)
        dv = jnp.zeros(queries.shape, F32)
        for head in range(2):
            head_queries = head_lanes(queries, head)
            head_dctx = head_lanes(dctx, head)
            prob = softmax_rows(head_queries * BF16(scale), key_rows, length)
            dprob = dot_nt(head_dctx, values)
            inner = jnp.sum(prob * dprob, -1, keepdims=True)
            dscores = (prob * (dprob - inner)).astype(BF16)
            dq = dq + dot(dscores, head_lanes(key_rows, head))
            dk = dk + dot_tn(dscores, head_queries)
            dv = dv + dot_tn(prob.astype(BF16), head_dctx)
        dq = (dq * scale).astype(BF16)
        dv = dv.astype(BF16)
        dqkv_ref[:, pl.ds(start, LANES)] = dq
        dqkv_ref[:, pl.ds(start + width, LANES)] = (dk * scale).astype(BF16)
        dqkv_ref[:, pl.ds(start + 2 * width, LANES)] = dv
        bsums_ref[0:1, pl.ds(start, LANES)] = jnp.sum(dq.astype(F32), 0, keepdims=True)
        bsums_ref[1:2, pl.ds(start, LANES)] = jnp.sum(dv.astype(F32), 0, keepdims=True)
        return carry

    lax.fori_loop(0, width // LANES, pair, 0)


def attention_backward(length, hid, own, peer, gain, dout, w_out, qkv):
    rows, model = hid.shape
    width = w_out.shape[0]
    shapes = [
        ((rows, model), F32),
        ((rows, model), BF16),
        ((rows, 3 * width), BF16),
        ((3, model), F32),
        ((2, width), F32),
    ]
    args = (hid, own, peer, gain, dout, w_out, qkv)
    return pl.pallas_call(
        functools.partial(attention_back_kernel, length),
        grid=(1,),
        in_specs=[whole(a.shape) for a in args],
        out_specs=[whole(s) for s, _ in shapes],
        out_shape=[jax.ShapeDtypeStruct(s, d) for s, d in shapes],
        scratch_shapes=[pltpu.VMEM((rows, width), BF16)],
        cost_estimate=cost(2 * rows * model * width + 40 * rows * rows * width, 20e6, rows * rows * 8),
        name="attention_backward",
    )(*args)


def output_kernel(hid0_ref, own0_ref, peer0_ref, hid1_ref, own1_ref, peer1_ref, bias_ref, out_ref):
    length = out_ref.shape[1]
    for image, refs in enumerate(((hid0_ref, own0_ref, peer0_ref), (hid1_ref, own1_ref, peer1_ref))):
        hid_ref, own_ref, peer_ref = refs
        total = hid_ref[0:length, :] + (own_ref[0:length, :] + peer_ref[0:length, :]) + bias_ref[...]
        out_ref[image] = total.astype(BF16)


def input_grad_kernel(
    x_ref, own0_ref, peer0_ref, dhid0_ref, own1_ref, peer1_ref, dhid1_ref, gain_ref, out_ref, sums_ref
):
    length = out_ref.shape[1]
    gains, shifts = 0.0, 0.0
    for image, refs in enumerate(((own0_ref, peer0_ref, dhid0_ref), (own1_ref, peer1_ref, dhid1_ref))):
        own_ref, peer_ref, dhid_ref = refs
        normed, inverse = normalise(x_ref[image].astype(F32))
        upstream = own_ref[0:length, :] + peer_ref[0:length, :]
        back = norm_backward(upstream, normed, inverse, gain_ref[...])
        out_ref[image] = (dhid_ref[0:length, :] + back).astype(BF16)
        gains = gains + jnp.sum(upstream * normed, 0, keepdims=True)
        shifts = shifts + jnp.sum(upstream, 0, keepdims=True)
    sums_ref[0:1, :] = gains
    sums_ref[1:2, :] = shifts


def simple_call(kernel, args, shapes, name):
    return pl.pallas_call(
        kernel,
        grid=(1,),
        in_specs=[whole(a.shape) for a in args],
        out_specs=[whole(s) for s, _ in shapes],
        out_shape=[jax.ShapeDtypeStruct(s, d) for s, d in shapes],
        cost_estimate=cost(1e7, sum(a.size * a.dtype.itemsize for a in args)),
        name=name,
    )(*args)


def swap(block, axis, bit):
    size = lax.axis_size(axis)
    return lax.ppermute(block, axis, [(i, i ^ bit) for i in range(size)])


def peer_of(partial, name):
    with jax.named_scope(name):
        return swap(partial, "tensor", 1)


def bits_of(size):
    return [1 << k for k in range(size.bit_length() - 1)]


def is_upper(bit):
    return (lax.axis_index("dp") & bit) != 0


def scatter_half(block, bit, name):
    upper = is_upper(bit)
    half = block.shape[0] // 2
    low, high = block[:half], block[half:]
    with jax.named_scope(name):
        arrived = swap(jnp.where(upper, low, high), "dp", bit)
    return jnp.where(upper, high, low) + arrived


def gather_half(block, bit, name):
    upper = is_upper(bit)
    with jax.named_scope(name):
        arrived = swap(block, "dp", bit)
    return jnp.concatenate(
        [jnp.where(upper, arrived, block), jnp.where(upper, block, arrived)], axis=0
    )


def dp_orders():
    bits = bits_of(lax.axis_size("dp"))
    return (bits, [bits[1], bits[0]] + bits[2:])


class Exchange:
    def __init__(self, left, right, tile, name):
        orders = dp_orders()
        upper = [is_upper(order[0]).astype(jnp.int32) for order in orders]
        send_tiles = jnp.stack([1 - upper[0], 3 - upper[1]])
        keep_tiles = jnp.stack([upper[0], 2 + upper[1]])
        self.name = name
        self.orders = orders
        self.send = weight_grad(send_tiles, left, right, tile, name + "_send")
        self.arrived = []
        for colour, order in enumerate(orders):
            with jax.named_scope(f"{name}_c{colour}_s0"):
                self.arrived.append(swap(self.send[colour], "dp", order[0]))
        self.keep = weight_grad(keep_tiles, left, right, tile, name + "_keep")

    def finish(self):
        results = []
        for colour, order in enumerate(self.orders):
            name = f"{self.name}_c{colour}"
            block = self.keep[colour] + self.arrived[colour]
            for step, bit in enumerate(order[1:], 1):
                block = scatter_half(block, bit, f"{name}_s{step}")
            for step, bit in reversed(list(enumerate(order))):
                block = gather_half(block, bit, f"{name}_g{step}")
            results.append(block)
        return jnp.concatenate(results, axis=0)


def dp_sum_small(vectors):
    flat = jnp.concatenate([v.reshape(-1) for v in vectors])
    packed = flat.reshape(-1, LANES)
    for bit in bits_of(lax.axis_size("dp")):
        with jax.named_scope(f"small_{bit}"):
            packed = packed + swap(packed, "dp", bit)
    packed = packed.reshape(-1)
    results, start = [], 0
    for v in vectors:
        results.append(packed[start : start + v.size].reshape(v.shape))
        start += v.size
    return results


def body(
    image_tokens,
    first_gain,
    first_shift,
    w_qkv,
    query_value_bias,
    w_out,
    out_bias,
    second_gain,
    second_shift,
    w_up,
    up_bias,
    w_down,
    down_bias,
    cotangent,
):
    images, length, model = image_tokens.shape
    width = w_qkv.shape[2]
    row = lambda v: v.reshape(1, -1)
    wqkv = w_qkv.reshape(model, 3 * width)
    bias = jnp.concatenate([query_value_bias[0], jnp.zeros((width,), F32), query_value_bias[1]])
    both = range(images)

    first = [
        attention_forward(i, image_tokens, row(first_gain), row(first_shift), wqkv, row(bias), w_out)
        for i in both
    ]
    xn, qkv, ctx, part = zip(*first)
    part_peer = [peer_of(part[i], f"attn_swap_{i}") for i in both]
    feed = [
        feed_forward(
            i, image_tokens, part[i], part_peer[i], row(out_bias), row(second_gain), row(second_shift),
            w_up, row(up_bias), w_down, cotangent,
        )
        for i in both
    ]
    hid, sn, act, dpre, dout, up_sums, down_sums = zip(*feed)
    down = Exchange(act, dout, act[0].shape[1] // 4, "down")
    up = Exchange(sn, dpre, model // 4, "up")
    d_second = [product(dpre[i], w_up, True, "d_second") for i in both]
    d_second_peer = [peer_of(d_second[i], f"second_swap_{i}") for i in both]
    back = [
        attention_backward(length, hid[i], d_second[i], d_second_peer[i], row(second_gain), dout[i], w_out, qkv[i])
        for i in both
    ]
    dhid, dlow, dqkv, sums, bias_sums = zip(*back)
    out = Exchange(ctx, dlow, width // 4, "out")
    joined = Exchange(xn, dqkv, model // 4, "qkv")
    d_first = [product(dqkv[i], wqkv, True, "d_first") for i in both]
    d_first_peer = [peer_of(d_first[i], f"first_swap_{i}") for i in both]
    branch = [product(act[i], w_down, False, "branch") for i in both]
    branch_peer = [peer_of(branch[i], f"branch_swap_{i}") for i in both]
    (layer_output,) = simple_call(
        output_kernel,
        (hid[0], branch[0], branch_peer[0], hid[1], branch[1], branch_peer[1], row(down_bias)),
        [(image_tokens.shape, BF16)],
        "layer_output",
    )
    grad_input, first_sums = simple_call(
        input_grad_kernel,
        (
            image_tokens, d_first[0], d_first_peer[0], dhid[0], d_first[1], d_first_peer[1], dhid[1],
            row(first_gain),
        ),
        [(image_tokens.shape, BF16), ((2, model), F32)],
        "input_grad",
    )
    sums = sums[0] + sums[1]
    small = dp_sum_small(
        (
            first_sums[0],
            first_sums[1],
            bias_sums[0] + bias_sums[1],
            sums[2],
            sums[0],
            sums[1],
            (up_sums[0] + up_sums[1]).reshape(-1),
            (down_sums[0] + down_sums[1]).reshape(-1),
        )
    )
    (
        grad_first_gain,
        grad_first_shift,
        grad_query_value_bias,
        grad_out_bias,
        grad_second_gain,
        grad_second_shift,
        grad_up_bias,
        grad_down_bias,
    ) = small
    grad_down = down.finish()
    grad_up = up.finish()
    grad_out = out.finish()
    grad_qkv = joined.finish().reshape(model, 3, width)
    return (
        layer_output,
        grad_input,
        grad_first_gain,
        grad_first_shift,
        grad_qkv,
        grad_query_value_bias,
        grad_out,
        grad_out_bias,
        grad_second_gain,
        grad_second_shift,
        grad_up,
        grad_up_bias,
        grad_down,
        grad_down_bias,
    )


def solution(mesh):
    in_specs = (
        P("dp", None, None),
        P(),
        P(),
        P(None, None, "tensor"),
        P(None, "tensor"),
        P("tensor", None),
        P(),
        P(),
        P(),
        P(None, "tensor"),
        P("tensor"),
        P("tensor", None),
        P(),
        P("dp", None, None),
    )
    out_specs = (
        P("dp", None, None),
        P("dp", None, None),
        P(),
        P(),
        P(None, None, "tensor"),
        P(None, "tensor"),
        P("tensor", None),
        P(),
        P(),
        P(),
        P(None, "tensor"),
        P("tensor"),
        P("tensor", None),
        P(),
    )
    return jax.shard_map(body, mesh=mesh, in_specs=in_specs, out_specs=out_specs, check_vma=False)
```

time: 1040 us -> 854 us (0.82)
  Pallas kernels: 0 us -> 216 us
  matrix products: 133 us -> 0 us
  waiting for transfers between devices: 587 us -> 459 us
  local copies, waits for them, and re-layouts: 145 us -> 40.8 us
  blocking collectives: 82 us -> 0 us
  starting transfers between devices: 0.16 us -> 62.5 us
  other arithmetic: 73.4 us -> 58.4 us
  between operations: 14.5 us -> 2.78 us
    psum x4 -> x0, waiting for transfers between devices: 587 us -> none  [the longest x1 554 us: body(): lax.psum((grad_first_gain, grad_first_shift, grad_qkv, grad_query_value_b...]
    ppermute x0 -> x76, waiting for transfers between devices: none -> 459 us  [swap(): return lax.ppermute(block, axis, [(i, i ^ bit) for i in range(size)])]
    pallas_call x0 -> x22, Pallas kernels: none -> 216 us  [the longest x8 59.4 us: weight_grad(): pl.pallas_call(weight_grad_kernel, grid_spec=pltpu.PrefetchScalarGridSpec...]
    dot_general x26 -> x0, matrix products: 133 us -> none  [the longest x1 13.6 us: body(): jnp.einsum('rd,rf->df', second_normed, d_pre, preferred_element_type=jnp....]
    psum x1 -> x0, blocking collectives: 82 us -> none  [body(): lax.psum((grad_first_gain, grad_first_shift, grad_qkv, grad_query_value_b...]
    ppermute x0 -> x76, starting transfers between devices: none -> 62.5 us  [swap(): return lax.ppermute(block, axis, [(i, i ^ bit) for i in range(size)])]
    reduce_sum x12 -> x0, other arithmetic: 38.8 us -> none  [the longest x2 11.7 us: norm_backward(): jnp.sum(upstream * normed, 0)]
    convert_element_type x7 -> x0, other arithmetic: 34.4 us -> none  [the longest x2 12.8 us: attend_backward(): d_scores = (prob_full * (d_prob - row_inner)).astype(jnp.bfloat16)]
  transfers between devices with their start and end apart: 4 -> 76, of which waited for: 3 -> 43; matrix products, arithmetic and copies ran while one was open for 10% -> 8% of each run, Pallas kernels for 0% -> 21%
where the time goes in v1:
time: 854 us; the launch traced here: 840 us
  waiting for transfers between devices  459 us (54%)
  Pallas kernels  216 us (25%)
  starting transfers between devices  62.5 us (7%)
  other arithmetic  58.4 us (7%)
  local copies, waits for them, and re-layouts  40.8 us (5%)
    ppermute x76, waiting for transfers between devices, swap(): return lax.ppermute(block, axis, [(i, i ^ bit) for i in range(size)])  459 us
    ppermute x76, starting transfers between devices, swap(): return lax.ppermute(block, axis, [(i, i ^ bit) for i in range(size)])  62.5 us
    pallas_call x8, Pallas kernels, weight_grad(): pl.pallas_call(weight_grad_kernel, grid_spec=pltpu.PrefetchScalarGridSpec...  59.4 us
    pallas_call x2, Pallas kernels, attention_backward(): pl.pallas_call(functools.partial(attention_back_kernel, length), grid=(1,...  45.9 us
    pallas_call x6, Pallas kernels, product(): pl.pallas_call(functools.partial(product_kernel, transposed), grid=(colum...  35.9 us
    pallas_call x2, Pallas kernels, attention_forward(): pl.pallas_call(functools.partial(attention_kernel, length), grid=(1,), in...  31.3 us
    unnamed x106, local copies, waits for them, and re-layouts  28.1 us
    pallas_call x2, Pallas kernels, feed_forward(): pl.pallas_call(feed_kernel, grid=(units // tile,), in_specs=[image_spec(t...  25.5 us
  transfers between devices with their start and end apart: 76, of which 43 were waited for; matrix products, arithmetic and copies ran while one was open for 8% of the time, Pallas kernels for 21%

profile of v1, /device:TPU:0, one launch (start us, length us, event | category | flops | bytes accessed | tf_op | source)
XLA Modules:
  0.0 840.1 jit_solution(15959156502933814784)
XLA Ops:
  11.3 15.5 %attention_forward.2 = (bf16[592,1024]{1,0:T(8,128)(2,1)}, bf16[592,1536]{1,0:T(8,128)(2,1)}, bf16[592,512]{1,0:T(8,128)(2,1)}, f32[592,1024]{1,0:T(8,128)}) custom-call(bf16[2,577,1024]{2,1,0:T(8,128)(2,1)} %copy.42.x_ref, f32[1,1024]{1,0:T(1,128)} %bitcast.57, f32[1,1024]{1,0:T(1,128)} %bitcast.62, bf16[1024,1536]{1,0:T(8,128)(2,1)} %copy.41.wqkv_ref.right_ref, ...), custom_call_target="tpu_custom_call" | custom-call | flops 5354029056 | bytes 12000000 | tf_op jit(solution)/shard_map/attention_forward/pallas_call | solution.py:115
  27.3 15.8 %attention_forward.3 = (bf16[592,1024]{1,0:T(8,128)(2,1)}, bf16[592,1536]{1,0:T(8,128)(2,1)}, bf16[592,512]{1,0:T(8,128)(2,1)}, f32[592,1024]{1,0:T(8,128)}) custom-call(bf16[2,577,1024]{2,1,0:T(8,128)(2,1)} %copy.42.x_ref, f32[1,1024]{1,0:T(1,128)} %bitcast.58, f32[1,1024]{1,0:T(1,128)} %bitcast.63, bf16[1024,1536]{1,0:T(8,128)(2,1)} %copy.41.wqkv_ref.right_ref, ...), custom_call_target="tpu_custom_call" | custom-call | flops 5354029056 | bytes 12000000 | tf_op jit(solution)/shard_map/attention_forward/pallas_call | solution.py:115
  45.8 12.9 %feed_forward.2 = (f32[592,1024]{1,0:T(8,128)}, bf16[592,1024]{1,0:T(8,128)(2,1)}, bf16[592,2048]{1,0:T(8,128)(2,1)}, bf16[592,2048]{1,0:T(8,128)(2,1)}, bf16[59...) custom-call(bf16[2,577,1024]{2,1,0:T(8,128)(2,1)} %copy.42.x_ref, ...), custom_call_target="tpu_custom_call" | custom-call | flops 4966055936 | bytes 25000000 | tf_op jit(solution)/shard_map/feed_forward/pallas_call | solution.py:170
  58.7 12.6 %feed_forward.3 = (f32[592,1024]{1,0:T(8,128)}, bf16[592,1024]{1,0:T(8,128)(2,1)}, bf16[592,2048]{1,0:T(8,128)(2,1)}, bf16[592,2048]{1,0:T(8,128)(2,1)}, bf16[59...) custom-call(bf16[2,577,1024]{2,1,0:T(8,128)(2,1)} %copy.42.x_ref, ...), custom_call_target="tpu_custom_call" | custom-call | flops 4966055936 | bytes 25000000 | tf_op jit(solution)/shard_map/feed_forward/pallas_call | solution.py:170
  140.9 33.2 %collective-permute-done.68 = f32[512,1024]{1,0:T(8,128)S(1)} collective-permute-done((f32[512,1024]{1,0:T(8,128)}, f32[512,1024]{1,0:T(8,128)S(1)}, u32[]{:S(2)}, u32[]{:S(2)}) %collective-permute-start.68) | collective-permute-done | bytes 2097184 | tf_op jit(solution)/shard_map/down_c1_s0/ppermute | solution.py:358
  191.7 23.2 %attention_backward.2 = (f32[592,1024]{1,0:T(8,128)}, bf16[592,1024]{1,0:T(8,128)(2,1)}, bf16[592,1536]{1,0:T(8,128)(2,1)}, f32[3,1024]{1,0:T(4,128)}, f32[2,512]{1,0:T(2,128)}) custom-call(f32[592,1024]{1,0:T(8,128)} %get-tuple-element.65.hid0_ref.hid_ref, f32[592,1024]{1,0:T(8,128)} %d_second.2.own_ref, f32[592,1024]{1,0:T(8,128)} %collective-permute-done.4.peer_ref, ...), custom_call_target="tpu_custom_call" | custom-call | flops 7798259712 | bytes 20000000 | tf_op jit(solution)/shard_map/attention_backward/pallas_call | solution.py:307
  215.4 22.7 %attention_backward.3 = (f32[592,1024]{1,0:T(8,128)}, bf16[592,1024]{1,0:T(8,128)(2,1)}, bf16[592,1536]{1,0:T(8,128)(2,1)}, f32[3,1024]{1,0:T(4,128)}, f32[2,512]{1,0:T(2,128)}) custom-call(f32[592,1024]{1,0:T(8,128)} %get-tuple-element.68.hid1_ref.hid_ref, f32[592,1024]{1,0:T(8,128)} %d_second.3.own_ref, f32[592,1024]{1,0:T(8,128)} %collective-permute-done.6.peer_ref, ...), custom_call_target="tpu_custom_call" | custom-call | flops 7798259712 | bytes 20000000 | tf_op jit(solution)/shard_map/attention_backward/pallas_call | solution.py:307
  299.0 15.7 %collective-permute-done.61 = f32[256,1024]{1,0:T(8,128)S(1)} collective-permute-done((f32[256,1024]{1,0:T(8,128)}, f32[256,1024]{1,0:T(8,128)S(1)}, u32[]{:S(2)}, u32[]{:S(2)}) %collective-permute-start.61) | collective-permute-done | bytes 1048608 | tf_op jit(solution)/shard_map/down_c0_s1/ppermute | solution.py:358
  316.7 20.7 %collective-permute-done.37 = f32[64,1024]{1,0:T(8,128)S(1)} collective-permute-done((f32[64,1024]{1,0:T(8,128)S(1)}, f32[64,1024]{1,0:T(8,128)S(1)}, u32[]{:S(2)}, u32[]{:S(2)}) %collective-permute-start.37) | collective-permute-done | bytes 262176 | tf_op jit(solution)/shard_map/out_c1_s1/ppermute | solution.py:358
  339.1 11.4 %collective-permute-done.29 = f32[64,1024]{1,0:T(8,128)S(1)} collective-permute-done((f32[64,1024]{1,0:T(8,128)S(1)}, f32[64,1024]{1,0:T(8,128)S(1)}, u32[]{:S(2)}, u32[]{:S(2)}) %collective-permute-start.29) | collective-permute-done | bytes 262176 | tf_op jit(solution)/shard_map/out_c0_s1/ppermute | solution.py:358
  399.9 12.5 %collective-permute-done.46 = f32[64,2048]{1,0:T(8,128)S(1)} collective-permute-done((f32[64,2048]{1,0:T(8,128)S(1)}, f32[64,2048]{1,0:T(8,128)S(1)}, u32[]{:S(2)}, u32[]{:S(2)}) %collective-permute-start.46) | collective-permute-done | bytes 524320 | tf_op jit(solution)/shard_map/up_c0_s2/ppermute | solution.py:358
  420.8 9.8 %collective-permute-done.62 = f32[128,1024]{1,0:T(8,128)S(1)} collective-permute-done((f32[128,1024]{1,0:T(8,128)S(1)}, f32[128,1024]{1,0:T(8,128)S(1)}, u32[]{:S(2)}, u32[]{:S(2)}) %collective-permute-start.62) | collective-permute-done | bytes 524320 | tf_op jit(solution)/shard_map/down_c0_s2/ppermute | solution.py:358
  437.3 12.5 %collective-permute-done.55 = f32[32,2048]{1,0:T(8,128)S(1)} collective-permute-done((f32[32,2048]{1,0:T(8,128)S(1)}, f32[32,2048]{1,0:T(8,128)S(1)}, u32[]{:S(2)}, u32[]{:S(2)}) %collective-permute-start.55) | collective-permute-done | bytes 262176 | tf_op jit(solution)/shard_map/up_c1_s3/ppermute | solution.py:358
  458.3 9.4 %collective-permute-done.47 = f32[32,2048]{1,0:T(8,128)S(1)} collective-permute-done((f32[32,2048]{1,0:T(8,128)S(1)}, f32[32,2048]{1,0:T(8,128)S(1)}, u32[]{:S(2)}, u32[]{:S(2)}) %collective-permute-start.47) | collective-permute-done | bytes 262176 | tf_op jit(solution)/shard_map/up_c0_s3/ppermute | solution.py:358
  481.7 14.0 %collective-permute-done.48 = f32[32,2048]{1,0:T(8,128)S(1)} collective-permute-done((f32[32,2048]{1,0:T(8,128)S(1)}, f32[32,2048]{1,0:T(8,128)S(1)}, u32[]{:S(2)}, u32[]{:S(2)}) %collective-permute-start.48) | collective-permute-done | bytes 262176 | tf_op jit(solution)/shard_map/up_c0_g3/ppermute | solution.py:358
  495.8 11.8 %collective-permute-done.72 = f32[64,1024]{1,0:T(8,128)S(1)} collective-permute-done((f32[64,1024]{1,0:T(8,128)S(1)}, f32[64,1024]{1,0:T(8,128)S(1)}, u32[]{:S(2)}, u32[]{:S(2)}) %collective-permute-start.72) | collective-permute-done | bytes 262176 | tf_op jit(solution)/shard_map/down_c1_g3/ppermute | solution.py:358
  526.4 11.1 %collective-permute-done.65 = f32[128,1024]{1,0:T(8,128)S(1)} collective-permute-done((f32[128,1024]{1,0:T(8,128)S(1)}, f32[128,1024]{1,0:T(8,128)S(1)}, u32[]{:S(2)}, u32[]{:S(2)}) %collective-permute-start.65) | collective-permute-done | bytes 524320 | tf_op jit(solution)/shard_map/down_c0_g2/ppermute | solution.py:358
  560.3 11.1 %input_grad.1 = (bf16[2,577,1024]{2,1,0:T(8,128)(2,1)}, f32[2,1024]{1,0:T(2,128)}) custom-call(bf16[2,577,1024]{2,1,0:T(8,128)(2,1)} %copy.42.x_ref, f32[592,1024]{1,0:T(8,128)} %d_first.2.own0_ref, f32[592,1024]{1,0:T(8,128)} %copy-done.25, f32[592,1024]{1,0:T(8,128)} %get-tuple-element.74.dhid0_ref, f32[592,1024]{1,0:T(8,128)} %d_first.3.own1_ref, ...), custom_call_target="tpu_custom_call" | custom-call | flops 10000000 | bytes 16916480 | tf_op jit(solution)/shard_map/input_grad/pallas_call | solution.py:345
  574.7 23.8 %collective-permute-done.8 = f32[72,128]{1,0:T(8,128)S(1)} collective-permute-done((f32[72,128]{1,0:T(8,128)S(1)}, f32[72,128]{1,0:T(8,128)S(1)}, u32[]{:S(2)}, u32[]{:S(2)}) %collective-permute-start.8) | collective-permute-done | bytes 36896 | tf_op jit(solution)/shard_map/small_1/ppermute | solution.py:358
  601.9 16.6 %collective-permute-done.9 = f32[72,128]{1,0:T(8,128)S(1)} collective-permute-done((f32[72,128]{1,0:T(8,128)S(1)}, f32[72,128]{1,0:T(8,128)S(1)}, u32[]{:S(2)}, u32[]{:S(2)}) %collective-permute-start.9) | collective-permute-done | bytes 36896 | tf_op jit(solution)/shard_map/small_2/ppermute | solution.py:358
  649.5 11.7 %collective-permute-done.23 = f32[32,1536]{1,0:T(8,128)S(1)} collective-permute-done((f32[32,1536]{1,0:T(8,128)S(1)}, f32[32,1536]{1,0:T(8,128)S(1)}, u32[]{:S(2)}, u32[]{:S(2)}) %collective-permute-start.23) | collective-permute-done | bytes 196640 | tf_op jit(solution)/shard_map/qkv_c1_s3/ppermute | solution.py:358
  661.2 9.6 %collective-permute-done.15 = f32[32,1536]{1,0:T(8,128)S(1)} collective-permute-done((f32[32,1536]{1,0:T(8,128)S(1)}, f32[32,1536]{1,0:T(8,128)S(1)}, u32[]{:S(2)}, u32[]{:S(2)}) %collective-permute-start.15) | collective-permute-done | bytes 196640 | tf_op jit(solution)/shard_map/qkv_c0_s3/ppermute | solution.py:358
  702.3 58.0 %collective-permute-done.26 = f32[128,1536]{1,0:T(8,128)S(1)} collective-permute-done((f32[128,1536]{1,0:T(8,128)S(1)}, f32[128,1536]{1,0:T(8,128)S(1)}, u32[]{:S(2)}, u32[]{:S(2)}) %collective-permute-start.26) | collective-permute-done | bytes 786464 | tf_op jit(solution)/shard_map/qkv_c1_g1/ppermute | solution.py:358
  761.5 38.1 %collective-permute-done.18 = f32[128,1536]{1,0:T(8,128)S(1)} collective-permute-done((f32[128,1536]{1,0:T(8,128)S(1)}, f32[128,1536]{1,0:T(8,128)S(1)}, u32[]{:S(2)}, u32[]{:S(2)}) %collective-permute-start.18) | collective-permute-done | bytes 786464 | tf_op jit(solution)/shard_map/qkv_c0_g1/ppermute | solution.py:358
  (394 shorter events, 403.4 us)
Async XLA Ops:
  91.5 82.7 %collective-permute-start.68 = (f32[512,1024]{1,0:T(8,128)}, f32[512,1024]{1,0:T(8,128)S(1)}, u32[]{:S(2)}, u32[]{:S(2)}) collective-permute-start(f32[512,1024]{1,0:T(8,128)} %get-tuple-element.113), channel_id=1, source_target_pairs={{0,4},{2,6},{4,0},{6,2},{8,12},{10,14},{12,8},{14,10},{16,20},{18,... | collective-permute-start | bytes 6291464 | tf_op jit(solution)/shard_map/down_c1_s0/ppermute | solution.py:358
  91.5 87.1 %collective-permute-start.44 = (f32[256,2048]{1,0:T(8,128)}, f32[256,2048]{1,0:T(8,128)}, u32[]{:S(2)}, u32[]{:S(2)}) collective-permute-start(f32[256,2048]{1,0:T(8,128)} %get-tuple-element.107), channel_id=1, source_target_pairs={{0,2},{2,0},{4,6},{6,4},{8,10},{10,8},{12,14},{14,12},{16,18},{18,... | collective-permute-start | bytes 6291464 | tf_op jit(solution)/shard_map/up_c0_s0/ppermute | solution.py:358
  94.1 90.1 %collective-permute-start.60 = (f32[512,1024]{1,0:T(8,128)}, f32[512,1024]{1,0:T(8,128)}, u32[]{:S(2)}, u32[]{:S(2)}) collective-permute-start(f32[512,1024]{1,0:T(8,128)} %get-tuple-element.111), channel_id=1, source_target_pairs={{0,2},{2,0},{4,6},{6,4},{8,10},{10,8},{12,14},{14,12},{16,18},{18,... | collective-permute-start | bytes 6291464 | tf_op jit(solution)/shard_map/down_c0_s0/ppermute | solution.py:358
  100.5 89.7 %collective-permute-start.4 = (f32[592,1024]{1,0:T(8,128)}, f32[592,1024]{1,0:T(8,128)}, u32[]{:S(2)}, u32[]{:S(2)}) collective-permute-start(f32[592,1024]{1,0:T(8,128)} %d_second.2.own_ref), channel_id=1, source_target_pairs={{0,1},{1,0},{2,3},{3,2},{4,5},{5,4},{6,7},{7,6},{8,9},{9,8},{10,11... | collective-permute-start | bytes 7274504 | tf_op jit(solution)/shard_map/second_swap_0/ppermute | solution.py:358
  129.9 84.9 %collective-permute-start.6 = (f32[592,1024]{1,0:T(8,128)}, f32[592,1024]{1,0:T(8,128)}, u32[]{:S(2)}, u32[]{:S(2)}) collective-permute-start(f32[592,1024]{1,0:T(8,128)} %d_second.3.own_ref), channel_id=1, source_target_pairs={{0,1},{1,0},{2,3},{3,2},{4,5},{5,4},{6,7},{7,6},{8,9},{9,8},{10,11... | collective-permute-start | bytes 7274504 | tf_op jit(solution)/shard_map/second_swap_1/ppermute | solution.py:358
  174.2 73.6 %collective-permute-start.1 = (f32[592,1024]{1,0:T(8,128)}, f32[592,1024]{1,0:T(8,128)}, u32[]{:S(2)}, u32[]{:S(2)}) collective-permute-start(f32[592,1024]{1,0:T(8,128)} %branch.2.own0_ref), channel_id=1, source_target_pairs={{0,1},{1,0},{2,3},{3,2},{4,5},{5,4},{6,7},{7,6},{8,9},{9,8},{10,11... | collective-permute-start | bytes 7274504 | tf_op jit(solution)/shard_map/branch_swap_0/ppermute | solution.py:358
  178.6 69.2 %collective-permute-start.3 = (f32[592,1024]{1,0:T(8,128)}, f32[592,1024]{1,0:T(8,128)}, u32[]{:S(2)}, u32[]{:S(2)}) collective-permute-start(f32[592,1024]{1,0:T(8,128)} %branch.3.own1_ref), channel_id=1, source_target_pairs={{0,1},{1,0},{2,3},{3,2},{4,5},{5,4},{6,7},{7,6},{8,9},{9,8},{10,11... | collective-permute-start | bytes 7274504 | tf_op jit(solution)/shard_map/branch_swap_1/ppermute | solution.py:358
  184.1 108.8 %collective-permute-start.53 = (f32[128,2048]{1,0:T(8,128)}, f32[128,2048]{1,0:T(8,128)}, u32[]{:S(2)}, u32[]{:S(2)}) collective-permute-start(f32[128,2048]{1,0:T(8,128)} %slice_select_fusion.2), channel_id=1, source_target_pairs={{0,2},{2,0},{4,6},{6,4},{8,10},{10,8},{12,14},{14,12},{16,18},{18,... | collective-permute-start | bytes 3145736 | tf_op jit(solution)/shard_map/up_c1_s1/ppermute | solution.py:358
  190.1 107.1 %collective-permute-start.45 = (f32[128,2048]{1,0:T(8,128)}, f32[128,2048]{1,0:T(8,128)S(1)}, u32[]{:S(2)}, u32[]{:S(2)}) collective-permute-start(f32[128,2048]{1,0:T(8,128)} %slice_select_fusion.3), channel_id=1, source_target_pairs={{0,4},{2,6},{4,0},{6,2},{8,12},{10,14},{12,8},{14,10},{16,20},{18,... | collective-permute-start | bytes 3145736 | tf_op jit(solution)/shard_map/up_c0_s1/ppermute | solution.py:358
  214.8 80.2 %collective-permute-start.69 = (f32[256,1024]{1,0:T(8,128)}, f32[256,1024]{1,0:T(8,128)}, u32[]{:S(2)}, u32[]{:S(2)}) collective-permute-start(f32[256,1024]{1,0:T(8,128)} %slice_select_fusion), channel_id=1, source_target_pairs={{0,2},{2,0},{4,6},{6,4},{8,10},{10,8},{12,14},{14,12},{16,18},{18,... | collective-permute-start | bytes 3145736 | tf_op jit(solution)/shard_map/down_c1_s1/ppermute | solution.py:358
  291.5 266.4 %collective-permute-start.5 = (f32[592,1024]{1,0:T(8,128)}, f32[592,1024]{1,0:T(8,128)S(1)}, u32[]{:S(2)}, u32[]{:S(2)}) collective-permute-start(f32[592,1024]{1,0:T(8,128)} %d_first.2.own0_ref), channel_id=1, source_target_pairs={{0,1},{1,0},{2,3},{3,2},{4,5},{5,4},{6,7},{7,6},{8,9},{9,8},{10,11... | collective-permute-start | bytes 7274504 | tf_op jit(solution)/shard_map/first_swap_0/ppermute | solution.py:358
  292.9 175.8 %collective-permute-start.20 = (f32[256,1536]{1,0:T(8,128)S(1)}, f32[256,1536]{1,0:T(8,128)S(1)}, u32[]{:S(2)}, u32[]{:S(2)}) collective-permute-start(f32[256,1536]{1,0:T(8,128)S(1)} %copy-done.45), channel_id=1, source_target_pairs={{0,4},{2,6},{4,0},{6,2},{8,12},{10,14},{12,8},{14,10},{16,20},{18,... | collective-permute-start | bytes 4718600 | tf_op jit(solution)/shard_map/qkv_c1_s0/ppermute | solution.py:358
  295.1 175.0 %collective-permute-start.12 = (f32[256,1536]{1,0:T(8,128)S(1)}, f32[256,1536]{1,0:T(8,128)S(1)}, u32[]{:S(2)}, u32[]{:S(2)}) collective-permute-start(f32[256,1536]{1,0:T(8,128)S(1)} %copy-done.44), channel_id=1, source_target_pairs={{0,2},{2,0},{4,6},{6,4},{8,10},{10,8},{12,14},{14,12},{16,18},{18,... | collective-permute-start | bytes 4718600 | tf_op jit(solution)/shard_map/qkv_c0_s0/ppermute | solution.py:358
  458.3 100.6 %collective-permute-start.7 = (f32[592,1024]{1,0:T(8,128)S(1)}, f32[592,1024]{1,0:T(8,128)S(1)}, u32[]{:S(2)}, u32[]{:S(2)}) collective-permute-start(f32[592,1024]{1,0:T(8,128)S(1)} %copy-done.6), channel_id=1, source_target_pairs={{0,1},{1,0},{2,3},{3,2},{4,5},{5,4},{6,7},{7,6},{8,9},{9,8},{10,11... | collective-permute-start | bytes 7274504 | tf_op jit(solution)/shard_map/first_swap_1/ppermute | solution.py:358
  510.5 62.1 %collective-permute-start.21 = (f32[128,1536]{1,0:T(8,128)}, f32[128,1536]{1,0:T(8,128)}, u32[]{:S(2)}, u32[]{:S(2)}) collective-permute-start(f32[128,1536]{1,0:T(8,128)} %slice_select_fusion.4), channel_id=1, source_target_pairs={{0,2},{2,0},{4,6},{6,4},{8,10},{10,8},{12,14},{14,12},{16,18},{18,... | collective-permute-start | bytes 2359304 | tf_op jit(solution)/shard_map/qkv_c1_s1/ppermute | solution.py:358
  537.5 62.1 %collective-permute-start.13 = (f32[128,1536]{1,0:T(8,128)}, f32[128,1536]{1,0:T(8,128)}, u32[]{:S(2)}, u32[]{:S(2)}) collective-permute-start(f32[128,1536]{1,0:T(8,128)} %slice_select_fusion.5), channel_id=1, source_target_pairs={{0,4},{2,6},{4,0},{6,2},{8,12},{10,14},{12,8},{14,10},{16,20},{18,... | collective-permute-start | bytes 2359304 | tf_op jit(solution)/shard_map/qkv_c0_s1/ppermute | solution.py:358
  555.4 132.9 %collective-permute-start.58 = (f32[128,2048]{1,0:T(8,128)}, f32[128,2048]{1,0:T(8,128)}, u32[]{:S(2)}, u32[]{:S(2)}) collective-permute-start(f32[128,2048]{1,0:T(8,128)} %pad_maximum_fusion.11), channel_id=1, source_target_pairs={{0,2},{2,0},{4,6},{6,4},{8,10},{10,8},{12,14},{14,12},{16,18},{18,... | collective-permute-start | bytes 3145736 | tf_op jit(solution)/shard_map/up_c1_g1/ppermute | solution.py:358
  557.8 134.1 %collective-permute-start.50 = (f32[128,2048]{1,0:T(8,128)}, f32[128,2048]{1,0:T(8,128)}, u32[]{:S(2)}, u32[]{:S(2)}) collective-permute-start(f32[128,2048]{1,0:T(8,128)} %pad_maximum_fusion.10), channel_id=1, source_target_pairs={{0,4},{2,6},{4,0},{6,2},{8,12},{10,14},{12,8},{14,10},{16,20},{18,... | collective-permute-start | bytes 3145736 | tf_op jit(solution)/shard_map/up_c0_g1/ppermute | solution.py:358
  558.9 136.0 %collective-permute-start.74 = (f32[256,1024]{1,0:T(8,128)}, f32[256,1024]{1,0:T(8,128)}, u32[]{:S(2)}, u32[]{:S(2)}) collective-permute-start(f32[256,1024]{1,0:T(8,128)} %pad_maximum_fusion.13), channel_id=1, source_target_pairs={{0,2},{2,0},{4,6},{6,4},{8,10},{10,8},{12,14},{14,12},{16,18},{18,... | collective-permute-start | bytes 3145736 | tf_op jit(solution)/shard_map/down_c1_g1/ppermute | solution.py:358
  598.5 99.9 %collective-permute-start.66 = (f32[256,1024]{1,0:T(8,128)}, f32[256,1024]{1,0:T(8,128)S(1)}, u32[]{:S(2)}, u32[]{:S(2)}) collective-permute-start(f32[256,1024]{1,0:T(8,128)} %pad_maximum_fusion.12), channel_id=1, source_target_pairs={{0,4},{2,6},{4,0},{6,2},{8,12},{10,14},{12,8},{14,10},{16,20},{18,... | collective-permute-start | bytes 3145736 | tf_op jit(solution)/shard_map/down_c0_g1/ppermute | solution.py:358
  692.0 109.0 %collective-permute-start.59 = (f32[256,2048]{1,0:T(8,128)S(1)}, f32[256,2048]{1,0:T(8,128)S(1)}, u32[]{:S(2)}, u32[]{:S(2)}) collective-permute-start(f32[256,2048]{1,0:T(8,128)S(1)} %pad_maximum_fusion.5), channel_id=1, source_target_pairs={{0,4},{2,6},{4,0},{6,2},{8,12},{10,14},{12,8},{14,10},{16,20},{18,... | collective-permute-start | bytes 6291464 | tf_op jit(solution)/shard_map/up_c1_g0/ppermute | solution.py:358
  694.9 108.6 %collective-permute-start.51 = (f32[256,2048]{1,0:T(8,128)S(1)}, f32[256,2048]{1,0:T(8,128)S(1)}, u32[]{:S(2)}, u32[]{:S(2)}) collective-permute-start(f32[256,2048]{1,0:T(8,128)S(1)} %pad_maximum_fusion.4), channel_id=1, source_target_pairs={{0,2},{2,0},{4,6},{6,4},{8,10},{10,8},{12,14},{14,12},{16,18},{18,... | collective-permute-start | bytes 6291464 | tf_op jit(solution)/shard_map/up_c0_g0/ppermute | solution.py:358
  698.4 105.6 %collective-permute-start.75 = (f32[512,1024]{1,0:T(8,128)S(1)}, f32[512,1024]{1,0:T(8,128)S(1)}, u32[]{:S(2)}, u32[]{:S(2)}) collective-permute-start(f32[512,1024]{1,0:T(8,128)S(1)} %pad_maximum_fusion.7), channel_id=1, source_target_pairs={{0,4},{2,6},{4,0},{6,2},{8,12},{10,14},{12,8},{14,10},{16,20},{18,... | collective-permute-start | bytes 6291464 | tf_op jit(solution)/shard_map/down_c1_g0/ppermute | solution.py:358
  700.9 103.9 %collective-permute-start.67 = (f32[512,1024]{1,0:T(8,128)S(1)}, f32[512,1024]{1,0:T(8,128)S(1)}, u32[]{:S(2)}, u32[]{:S(2)}) collective-permute-start(f32[512,1024]{1,0:T(8,128)S(1)} %pad_maximum_fusion.6), channel_id=1, source_target_pairs={{0,2},{2,0},{4,6},{6,4},{8,10},{10,8},{12,14},{14,12},{16,18},{18,... | collective-permute-start | bytes 6291464 | tf_op jit(solution)/shard_map/down_c0_g0/ppermute | solution.py:358
  (98 other events, 1410.2 us)
